TPU v7x, 32 devices: a whole 2x2x4 slice. The times are simulated.
32 devices in a mesh: ctx: 8 (over z, y), tile: 4 (over x, core).
Axes of the slice: x: 2, y: 2, z: 4, core: 2. Of those that a mesh axis runs over, the one named last changes fastest.
Arguments:
- masks: bfloat16 [16, 512, 512], P('ctx', 'tile'), may hold values from 0 to 1
- blur_rows: bfloat16 [512, 512], replicated, may hold values from -0.25 to 0.25
- blur_cols: bfloat16 [512, 512], replicated, may hold values from -0.25 to 0.25
- pupils: float32 [6, 64, 128], replicated, may hold values from -5 to 5
- targets: bfloat16 [16, 512, 512], P('ctx', 'tile'), may hold values from 0 to 1
- context_masters: int32 [16, 12], P('ctx'), may hold values from 0 to 15, as said below
- offsets: int32 [16, 12, 2], P('ctx'), may hold values from 0 to 511
Outputs:
- resist: bfloat16 [16, 512, 512], P('ctx', 'tile')
- mask_grad: float32 [16, 512, 512], P('ctx', 'tile')
Inputs may be any that keep to these rules, and one draw needn't show every extreme that they name: `context_masters`: master m lies on ctx index m // 2. Among the masters named by the 2 contexts of one ctx index there is at most one lying on any one ctx index; a master may be named several times.
All inputs are finite; a program needn't handle non-finite values.
Results may differ from a plain program's by a relative error of at most 0.019.
Values may be sent and summed in bfloat16 or wider, within the bound.
No kernel may reach another device: no remote copies, remote signals or barrier semaphores. Data moves between devices by JAX's collectives and lax.ppermute only.
A program may use at most 64 MiB of HBM per device.

v0:
```python
import math
import jax
import jax.numpy as jnp
from jax import lax
from jax.sharding import PartitionSpec as P

STEEPNESS = 4.0
THRESHOLD = 1.0


def build_tables(extent, mode_count):
    frequency = (jnp.arange(mode_count, dtype=jnp.int32) - mode_count // 2) % extent
    positions = jnp.arange(extent, dtype=jnp.int32)
    windings = frequency[:, None] * positions[None, :] % extent
    angles = windings.astype(jnp.float32) * (2.0 * math.pi / extent)
    scale_factor = 1.0 / math.sqrt(extent)
    cosine_table = jnp.cos(angles) * scale_factor
    sine_table = jnp.sin(angles) * scale_factor
    row_real = cosine_table.astype(jnp.bfloat16)
    row_imag = (-sine_table).astype(jnp.bfloat16)
    col_fwd = jnp.concatenate([cosine_table.T, -sine_table.T], axis=1).astype(jnp.bfloat16)
    inverse_big = jnp.concatenate(
        [
            jnp.concatenate([cosine_table, sine_table], axis=1),
            jnp.concatenate([-sine_table, cosine_table], axis=1),
        ],
        axis=0,
    ).astype(jnp.bfloat16)
    back_real = cosine_table.T.astype(jnp.bfloat16)
    back_imag = sine_table.T.astype(jnp.bfloat16)
    adjoint_big = jnp.concatenate(
        [
            jnp.concatenate([cosine_table.T, -sine_table.T], axis=1),
            jnp.concatenate([sine_table.T, cosine_table.T], axis=1),
        ],
        axis=0,
    ).astype(jnp.bfloat16)
    return (row_real, row_imag, col_fwd, inverse_big, back_real, back_imag, adjoint_big)


def complex_left(left_real, left_imag, values):
    width = values.shape[-1] // 2
    real_lead = jnp.einsum("ux,...xv->...uv", left_real, values, preferred_element_type=jnp.float32)
    imag_lead = jnp.einsum("ux,...xv->...uv", left_imag, values, preferred_element_type=jnp.float32)
    return jnp.concatenate(
        [
            real_lead[..., :width] - imag_lead[..., width:],
            real_lead[..., width:] + imag_lead[..., :width],
        ],
        axis=-1,
    )


def complex_times(factor, values, conjugate):
    width = values.shape[-1] // 2
    factor_real = factor[..., :width]
    factor_imag = factor[..., width:]
    if conjugate:
        factor_imag = -factor_imag
    values_real = values[..., :width]
    values_imag = values[..., width:]
    return jnp.concatenate(
        [
            factor_real * values_real - factor_imag * values_imag,
            factor_real * values_imag + factor_imag * values_real,
        ],
        axis=-1,
    )


def phase_table(shifts, row_begin, band_rows, mode_count, extent):
    freq_u = (jnp.arange(band_rows, dtype=jnp.int32) + row_begin - mode_count // 2) % extent
    freq_v = (jnp.arange(mode_count, dtype=jnp.int32) - mode_count // 2) % extent
    windings = (
        freq_u[None, :, None] * shifts[:, 0][:, None, None]
        + freq_v[None, None, :] * shifts[:, 1][:, None, None]
    ) % extent
    angles = windings.astype(jnp.float32) * (2.0 * math.pi / extent)
    return jnp.concatenate([jnp.cos(angles), -jnp.sin(angles)], axis=-1)


def image_adjoint(
    spectrum, target, pupils, back_real, back_imag, row_real, row_imag, inverse_big, adjoint_big
):
    amplitude = complex_times(pupils, spectrum[None], False).astype(jnp.bfloat16)
    spread = jnp.einsum(
        "kuv,vy->kuy", amplitude, inverse_big, preferred_element_type=jnp.float32
    ).astype(jnp.bfloat16)
    field = complex_left(back_real, back_imag, spread)
    width = field.shape[-1] // 2
    field_real = field[..., :width]
    field_imag = field[..., width:]
    intensity = jnp.sum(field_real * field_real + field_imag * field_imag, axis=0)
    resist = jax.nn.sigmoid(STEEPNESS * (intensity - THRESHOLD))
    slope_term = (resist - target.astype(jnp.float32)) * STEEPNESS * resist * (1.0 - resist)
    pull_back = jnp.concatenate(
        [2.0 * slope_term * field_real, 2.0 * slope_term * field_imag], axis=-1
    ).astype(jnp.bfloat16)
    folded = jnp.einsum(
        "kxy,yv->kxv", pull_back, adjoint_big, preferred_element_type=jnp.float32
    ).astype(jnp.bfloat16)
    grad_amp = complex_left(row_real, row_imag, folded)
    grad_spec = jnp.sum(complex_times(pupils, grad_amp, True), axis=0)
    return (resist.astype(jnp.bfloat16), grad_spec)


def local(masks, blur_rows, blur_cols, pupils, targets, context_masters, offsets):
    ctx_count = lax.axis_size("ctx")
    owned, row_count, extent = masks.shape
    mode_count = pupils.shape[1]
    context_count = context_masters.shape[0]
    source_count = context_masters.shape[1]
    tile_pos = lax.axis_index("tile")
    row_start = tile_pos * row_count
    row_real, row_imag, col_fwd, inverse_big, back_real, back_imag, adjoint_big = build_tables(
        extent, mode_count
    )
    own_row_real = lax.dynamic_slice_in_dim(row_real, row_start, row_count, 1)
    own_row_imag = lax.dynamic_slice_in_dim(row_imag, row_start, row_count, 1)
    own_back_real = lax.dynamic_slice_in_dim(back_real, row_start, row_count, 0)
    own_back_imag = lax.dynamic_slice_in_dim(back_imag, row_start, row_count, 0)
    own_blur = lax.dynamic_slice_in_dim(blur_rows, row_start, row_count, 0)
    own_blur_cols = lax.dynamic_slice_in_dim(blur_rows, row_start, row_count, 1)
    owners = (context_masters // owned).reshape(-1)
    local_index = (context_masters % owned).reshape(-1)
    slot_index = jnp.arange(ctx_count, dtype=jnp.int32)
    owner_match = owners[:, None] == slot_index[None, :]
    wanted = jnp.max(jnp.where(owner_match, local_index[:, None] + 1, 0), axis=0)
    asked_for = lax.all_to_all(wanted[:, None], "ctx", split_axis=0, concat_axis=0, tiled=True)[
        :, 0
    ]
    chosen = asked_for[:, None] == jnp.arange(owned, dtype=jnp.int32)[None, :] + 1
    half_blur = jnp.einsum(
        "mxy,zy->mxz", masks, blur_cols, preferred_element_type=jnp.float32
    ).astype(jnp.bfloat16)
    weights = own_blur
    blurred = jnp.einsum(
        "xj,mjz->mxz",
        weights,
        lax.all_gather(half_blur, "tile", axis=1, tiled=True),
        preferred_element_type=jnp.float32,
    ).astype(jnp.bfloat16)
    column = jnp.einsum("mxy,yv->mxv", blurred, col_fwd, preferred_element_type=jnp.float32).astype(
        jnp.bfloat16
    )
    partial_value = complex_left(own_row_real, own_row_imag, column)
    spectra = lax.psum(partial_value.astype(jnp.bfloat16), "tile")
    outgoing = jnp.einsum(
        "dm,muv->duv", chosen.astype(jnp.bfloat16), spectra, preferred_element_type=jnp.float32
    ).astype(jnp.bfloat16)
    incoming = lax.all_to_all(outgoing, "ctx", split_axis=0, concat_axis=0, tiled=True)
    flat_shift = offsets.reshape(-1, 2)
    picked = jnp.take(incoming, owners, axis=0).astype(jnp.float32)
    turned = complex_times(
        phase_table(flat_shift, 0, mode_count, mode_count, extent), picked, False
    )
    context_spec = jnp.sum(
        turned.reshape(context_count, source_count, mode_count, 2 * mode_count), axis=1
    )

    def one_context(inputs):
        spectrum, target = inputs
        return image_adjoint(
            spectrum,
            target,
            pupils,
            own_back_real,
            own_back_imag,
            own_row_real,
            own_row_imag,
            inverse_big,
            adjoint_big,
        )

    resist, grad_part = lax.map(one_context, (context_spec, targets))
    grad_ctx = lax.psum(grad_part.astype(jnp.bfloat16), "tile").astype(jnp.float32)
    band_start = 0
    repeated = jnp.repeat(grad_ctx, source_count, axis=0)
    back_turn = complex_times(
        phase_table(flat_shift, band_start, mode_count, mode_count, extent), repeated, True
    )
    returned = jnp.einsum(
        "rd,ruv->duv", owner_match.astype(jnp.float32), back_turn, precision=lax.Precision.HIGHEST
    )
    arrived = lax.all_to_all(
        returned.astype(jnp.bfloat16), "ctx", split_axis=0, concat_axis=0, tiled=True
    ).astype(returned.dtype)
    master_grad = jnp.einsum(
        "dm,duv->muv", chosen.astype(jnp.float32), arrived, precision=lax.Precision.HIGHEST
    ).astype(jnp.bfloat16)
    lifted = jnp.einsum(
        "muv,vy->muy", master_grad, inverse_big, preferred_element_type=jnp.float32
    ).astype(jnp.bfloat16)
    surface = (
        jnp.einsum(
            "xu,muy->mxy", own_back_real, lifted[..., :extent], preferred_element_type=jnp.float32
        )
        - jnp.einsum(
            "xu,muy->mxy", own_back_imag, lifted[..., extent:], preferred_element_type=jnp.float32
        )
    ).astype(jnp.bfloat16)
    settled = jnp.einsum(
        "mxy,yz->mxz", surface, blur_cols, preferred_element_type=jnp.float32
    ).astype(jnp.bfloat16)
    weights = own_blur_cols
    mask_grad = jnp.einsum(
        "jx,mjz->mxz",
        weights,
        lax.all_gather(settled, "tile", axis=1, tiled=True),
        preferred_element_type=jnp.float32,
    )
    return (resist, mask_grad)


def solution(mesh):
    placed = (
        P("ctx", "tile", None),
        P(),
        P(),
        P(),
        P("ctx", "tile", None),
        P("ctx", None),
        P("ctx", None, None),
    )
    return jax.shard_map(
        local,
        mesh=mesh,
        in_specs=placed,
        out_specs=(P("ctx", "tile", None), P("ctx", "tile", None)),
        check_vma=False,
    )
```

profile of v0, /device:TPU:0, one launch (start us, length us, event | category | flops | bytes accessed | tf_op | source)
XLA Modules:
  0.0 133.8 jit_solution(16642103256916884030)
XLA Ops:
  7.2 1.0 copy-done
  8.2 2.0 %convolution_convert_fusion.4 = bf16[2,128,512]{2,1,0:T(8,128)(2,1)} fusion(bf16[2,128,512]{2,1,0:T(8,128)(2,1)} %param.9, bf16[512,512]{1,0:T(8,128)(2,1)S(1)} %copy-done), kind=kOutput, calls=%fused_computation.57 | convolution fusion | flops 134348800 | bytes 1048576 | tf_op jit(solution)/shard_map/mxy,zy->mxz/dot_general | solution.py:133
  10.2 0.7 and_select_fusion.1
  11.3 0.7 copy.75
  11.9 7.3 %all-to-all-start = ((s32[8,1,1]{2,1,0:T(1,128)}), s32[8,1,1]{2,1,0:T(1,128)S(1)}, u32[]{:S(2)}, u32[]{:S(2)}) async-start(s32[8,1,1]{2,1,0:T(1,128)} %copy.75), calls=%async_computation | async-start | bytes 8192 | tf_op jit(solution)/shard_map/all_to_all | solution.py:129
  19.3 0.7 copy.73
  20.1 1.1 fusion.45
  21.6 0.6 fusion.65
  22.2 1.1 cosine_multiply_fusion
  23.7 2.0 %all-to-all-done = s32[8,1,1]{2,1,0:T(1,128)S(1)} async-done(((s32[8,1,1]{2,1,0:T(1,128)}), s32[8,1,1]{2,1,0:T(1,128)S(1)}, u32[]{:S(2)}, u32[]{:S(2)}) %all-to-all-start) | async-done | bytes 64 | tf_op jit(solution)/shard_map/all_to_all | solution.py:129
  25.7 0.2 reduce
  26.0 3.9 %all-gather.3.cloned.1.call-done = bf16[2,512,512]{2,1,0:T(8,128)(2,1)} async-done(((bf16[2,128,512]{2,1,0:T(8,128)(2,1)}), bf16[2,512,512]{2,1,0:T(8,128)(2,1)}) %all-gather.3.cloned.1.call-update) | async-done | bytes 1048592 | tf_op jit(solution)/shard_map/all_gather | solution.py:140
  29.9 1.9 %fusion.26 = bf16[2,128,128]{2,1,0:T(8,128)(2,1)S(1)} fusion(bf16[2,512,512]{2,1,0:T(8,128)(2,1)} %all-gather.3.cloned.1.call-done, bf16[512,128]{1,0:T(8,128)(2,1)S(1)} %maximum_convert_fusion, bf16[512,512]{1,0:T(8,128)(2,1)S(1)} %copy-done.5, s32[]{:T(128)S(6)} %select_n.140), kind=kOutput, calls=%fused_computation.65 | convolution fusion | flops 167936000 | bytes 1376260 | tf_op jit(solution)/shard_map/mxy,yv->mxv/dot_general | solution.py:143
  31.8 0.1 convolution_bitcast_fusion.6
  31.9 0.1 convolution_bitcast_fusion.5
  32.3 10.4 %psum.14 = bf16[2,64,128]{2,1,0:T(8,128)(2,1)S(1)} all-reduce(bf16[2,64,128]{2,1,0:T(8,128)(2,1)S(1)} %pad_maximum_fusion.1), channel_id=1, replica_groups=mesh['ctx'=8,'tile'=4] {'tile'}, use_global_device_ids=true, to_apply=%region_1.2 | all-reduce | flops 16384 | bytes 65536 | tf_op jit(solution)/shard_map/psum | solution.py:147
  42.7 0.3 convolution_convert_fusion.5
  43.0 0.7 copy.79
  43.6 5.7 %all-to-all-start.1 = ((bf16[8,64,128]{2,1,0:T(8,128)(2,1)}), bf16[8,64,128]{2,1,0:T(8,128)(2,1)S(1)}, u32[]{:S(2)}, u32[]{:S(2)}) async-start(bf16[8,64,128]{2,1,0:T(8,128)(2,1)} %copy.79), calls=%async_computation.1 | async-start | bytes 262144 | tf_op jit(solution)/shard_map/all_to_all | solution.py:151
  49.5 7.2 %all-to-all-done.1 = bf16[8,64,128]{2,1,0:T(8,128)(2,1)S(1)} async-done(((bf16[8,64,128]{2,1,0:T(8,128)(2,1)}), bf16[8,64,128]{2,1,0:T(8,128)(2,1)S(1)}, u32[]{:S(2)}, u32[]{:S(2)}) %all-to-all-start.1) | async-done | bytes 131104 | tf_op jit(solution)/shard_map/all_to_all | solution.py:151
  56.7 0.6 gather_fusion
  57.3 0.3 fusion.35
  57.6 4.6 %multiply_subtract_fusion.2 = (f32[24,64,64]{2,0,1:T(8,128)S(1)}, f32[24,64,64]{2,0,1:T(8,128)S(1)}) fusion(f32[24,64,128]{2,0,1:T(8,128)S(1)} %fusion.35, s32[24,64]{1,0:T(8,128)S(1)} %get-tuple-element.289, s32[24,64]{0,1:T(8,128)S(1)} %copy.74), kind=kLoop, calls=%fused_computation.79 | loop fusion | flops 2064384 | bytes 1585152 | tf_op jit(solution)/shard_map/sub | solution.py:64
  62.2 0.3 pad_maximum_fusion
  62.5 0.2 copy.81
  62.7 0.7 copy-done.4
  63.4 19.3 %while.14 = (s32[]{:T(128)}, bf16[2,128,512]{2,1,0:T(8,128)(2,1)}, bf16[2,64,128]{2,1,0:T(8,128)(2,1)S(1)}, f32[6,64,128]{2,1,0:T(8,128)S(1)}, f32[2,64,128]{2,1...) while((s32[]{:T(128)}, bf16[2,128,512]{2,1,0:T(8,128)(2,1)}, ...), condition=%wide.region_6.7_spmd, body=%wide.region_3.6_spmd.sunk | while | flops 538632192 | bytes 57360672 | solution.py:175
  63.5 0.1 subtract_convert_fusion.2
  63.6 0.4 convolution_convert_fusion.9
  64.0 0.6 convolution_bitcast_fusion.11
  64.7 0.6 convolution_bitcast_fusion.12
  65.3 1.0 copy-done.1
  66.3 0.4 add_reduce_fusion.2
  66.8 1.2 copy-done.2
  68.4 0.1 fusion.130
  68.5 3.3 %multiply_convert_fusion.4 = (bf16[6,128,512]{1,2,0:T(8,128)(2,1)S(1)}, bf16[6,128,512]{1,2,0:T(8,128)(2,1)S(1)}) fusion(f32[128,512]{0,1:T(8,128)S(1)} %fusion.130, f32[6,128,1024]{1,2,0:T(8,128)} %copy-done.1, f32[6,128,1024]{1,2,0:T(8,128)} %copy-done.2), kind=kLoop, calls=%fused_computation.10.clone.1 | loop fusion | flops 2359296 | bytes 8126464 | tf_op jit(solution)/shard_map/convert
  71.8 0.6 fusion.131
  72.4 0.1 convolution_bitcast_fusion.13
  72.6 0.2 convolution_bitcast_fusion.14
  72.7 0.2 multiply_subtract_fusion.4
  73.2 0.1 subtract_convert_fusion.2
  73.3 0.4 convolution_convert_fusion.9
  73.7 0.6 convolution_bitcast_fusion.11
  74.4 0.6 convolution_bitcast_fusion.12
  75.0 1.0 copy-done.1
  76.0 0.4 add_reduce_fusion.2
  76.4 1.2 copy-done.2
  78.2 3.3 %multiply_convert_fusion.4 = (bf16[6,128,512]{1,2,0:T(8,128)(2,1)S(1)}, bf16[6,128,512]{1,2,0:T(8,128)(2,1)S(1)}) fusion(f32[128,512]{0,1:T(8,128)S(1)} %fusion.130, f32[6,128,1024]{1,2,0:T(8,128)} %copy-done.1, f32[6,128,1024]{1,2,0:T(8,128)} %copy-done.2), kind=kLoop, calls=%fused_computation.10.clone.1 | loop fusion | flops 2359296 | bytes 8126464 | tf_op jit(solution)/shard_map/convert
  81.5 0.6 fusion.131
  82.1 0.1 convolution_bitcast_fusion.13
  82.3 0.2 convolution_bitcast_fusion.14
  82.4 0.2 multiply_subtract_fusion.4
  82.8 10.4 %psum.15 = bf16[2,64,128]{2,1,0:T(8,128)(2,1)S(1)} all-reduce(bf16[2,64,128]{2,1,0:T(8,128)(2,1)S(1)} %get-tuple-element.159), channel_id=1, replica_groups=mesh['ctx'=8,'tile'=4] {'tile'}, use_global_device_ids=true, to_apply=%region_7.8 | all-reduce | flops 16384 | bytes 65536 | tf_op jit(solution)/shard_map/psum | solution.py:176
  93.3 0.3 fusion.94
  93.6 3.7 %multiply_subtract_fusion.1 = (f32[24,64,64]{2,0,1:T(8,128)S(1)}, f32[24,64,64]{2,0,1:T(8,128)S(1)}) fusion(f32[24,64,64]{2,1,0:T(8,128)S(1)} %get-tuple-element.276, f32[24,64,64]{2,1,0:T(8,128)S(1)} %get-tuple-element.275, s32[24,64]{1,0:T(8,128)S(1)} %get-tuple-element.289, s32[24,64]{0,1:T(8,128)S(1)} %copy.74), kind=kLoop, calls=%fused_computation.77 | loop fusion | flops 1966080 | bytes 1585152 | tf_op jit(solution)/shard_map/sub | solution.py:64
  97.3 0.5 convolution_convert_fusion.6
  97.8 9.9 %all_to_all.19 = bf16[8,64,128]{2,1,0:T(8,128)(2,1)S(1)} all-to-all(bf16[8,64,128]{2,1,0:T(8,128)(2,1)S(1)} %copy.87), channel_id=1, replica_groups=mesh['ctx'=8,'tile'=4] {'ctx'}, dimensions={0} | all-to-all | bytes 262144 | tf_op jit(solution)/shard_map/all_to_all | solution.py:185
  107.7 0.2 convolution_convert_fusion.7
  108.0 0.2 convolution_convert_fusion.2
  108.2 0.3 fusion.52
  108.5 1.3 %convolution_convert_fusion.1 = bf16[2,128,512]{2,1,0:T(8,128)(2,1)} fusion(f32[2,512,128]{2,1,0:T(8,128)S(1)} %fusion.52, bf16[512,512]{1,0:T(8,128)(2,1)S(1)} %copy-done, bf16[2,64,1024]{2,1,0:T(8,128)(2,1)S(1)} %convolution_convert_fusion.2, bf16[128,64]{1,0:T(8,128)(2,1)S(1)} %constant_dynamic-slice_fusion.1), kind=kOutput, calls=%fused_computation.54 | convolution fusion | flops 151388160 | bytes 1474560 | tf_op jit(solution)/shard_map/mxy,yz->mxz/dot_general | solution.py:202
  109.8 14.5 %all-gather.5.cloned.1.call-done = bf16[2,512,512]{2,1,0:T(8,128)(2,1)} async-done(((bf16[2,128,512]{2,1,0:T(8,128)(2,1)}), bf16[2,512,512]{2,1,0:T(8,128)(2,1)}) %all-gather.5.cloned.1.call-update) | async-done | bytes 1048592 | tf_op jit(solution)/shard_map/all_gather | solution.py:209
  124.3 1.7 %convolution_bitcast_fusion.4 = f32[2,128,512]{1,2,0:T(8,128)S(1)} fusion(bf16[2,512,512]{2,1,0:T(8,128)(2,1)} %all-gather.5.cloned.1.call-done, bf16[512,512]{1,0:T(8,128)(2,1)S(1)} %copy-done.5, s32[]{:T(128)S(6)} %select_n.140), kind=kOutput, calls=%fused_computation.51 | convolution fusion | flops 134217728 | bytes 1703940 | tf_op jit(solution)/shard_map/jx,mjz->mxz/dot_general | solution.py:206
  126.0 1.0 copy.95
  (66 shorter events, 2.9 us)
Async XLA Ops:
  7.2 1.0 copy-start
  7.2 22.7 %all-gather.3.cloned.1.call-start = ((), (), s32[]{:S(2)}) async-start(), calls=%async_computation.3 | async-start | bytes 1310720 | tf_op jit(solution)/shard_map/all_gather | solution.py:140
  10.2 19.7 %copy-start.5 = (bf16[512,512]{1,0:T(8,128)(2,1)S(1)}, bf16[512,512]{1,0:T(8,128)(2,1)}, u32[]{:S(2)}) copy-start(bf16[512,512]{1,0:T(8,128)(2,1)} %param.10) | copy-start | bytes 1572868
  11.9 13.8 %all-to-all-start = ((s32[8,1,1]{2,1,0:T(1,128)}), s32[8,1,1]{2,1,0:T(1,128)S(1)}, u32[]{:S(2)}, u32[]{:S(2)}) async-start(s32[8,1,1]{2,1,0:T(1,128)} %copy.75), calls=%async_computation | async-start | bytes 8192 | tf_op jit(solution)/shard_map/all_to_all | solution.py:129
  23.6 25.8 %copy-start.3 = (f32[6,64,128]{2,1,0:T(8,128)S(1)}, f32[6,64,128]{2,1,0:T(8,128)}, u32[]{:S(2)}) copy-start(f32[6,64,128]{2,1,0:T(8,128)} %param.12) | copy-start | bytes 589828
  43.6 13.0 %all-to-all-start.1 = ((bf16[8,64,128]{2,1,0:T(8,128)(2,1)}), bf16[8,64,128]{2,1,0:T(8,128)(2,1)S(1)}, u32[]{:S(2)}, u32[]{:S(2)}) async-start(bf16[8,64,128]{2,1,0:T(8,128)(2,1)} %copy.79), calls=%async_computation.1 | async-start | bytes 262144 | tf_op jit(solution)/shard_map/all_to_all | solution.py:151
  49.3 75.0 %all-gather.5.cloned.1.call-start = ((), (), s32[]{:S(2)}) async-start(), calls=%async_computation.4 | async-start | bytes 1310720 | tf_op jit(solution)/shard_map/all_gather | solution.py:209
  62.5 1.0 copy-start.4
  64.7 1.6 %copy-start.1 = (f32[6,128,1024]{1,2,0:T(8,128)}, f32[6,128,1024]{1,2,0:T(8,128)S(1)}, u32[]{:S(2)}) copy-start(f32[6,128,1024]{1,2,0:T(8,128)S(1)} %convolution_bitcast_fusion.11) | copy-start | bytes 9437188 | tf_op jit(solution)/shard_map/while
  66.3 1.7 %copy-start.2 = (f32[6,128,1024]{1,2,0:T(8,128)}, f32[6,128,1024]{1,2,0:T(8,128)S(1)}, u32[]{:S(2)}) copy-start(f32[6,128,1024]{1,2,0:T(8,128)S(1)} %convolution_bitcast_fusion.12) | copy-start | bytes 9437188 | tf_op jit(solution)/shard_map/while
  66.3 1.9 %copy-start.6 = (bf16[2,128,512]{2,1,0:T(8,128)(2,1)S(1)}, bf16[2,128,512]{2,1,0:T(8,128)(2,1)}, u32[]{:S(2)}) copy-start(bf16[2,128,512]{2,1,0:T(8,128)(2,1)} %get-tuple-element.410) | copy-start | bytes 786436 | tf_op jit(solution)/shard_map/while
  68.2 3.6 %copy-start.7 = (bf16[2,128,512]{2,1,0:T(8,128)(2,1)}, bf16[2,128,512]{2,1,0:T(8,128)(2,1)S(1)}, u32[]{:S(2)}) copy-start(bf16[2,128,512]{2,1,0:T(8,128)(2,1)S(1)} %get-tuple-element.426) | copy-start | bytes 786436 | tf_op jit(solution)/shard_map/while
  74.4 1.6 %copy-start.1 = (f32[6,128,1024]{1,2,0:T(8,128)}, f32[6,128,1024]{1,2,0:T(8,128)S(1)}, u32[]{:S(2)}) copy-start(f32[6,128,1024]{1,2,0:T(8,128)S(1)} %convolution_bitcast_fusion.11) | copy-start | bytes 9437188 | tf_op jit(solution)/shard_map/while
  76.0 1.7 %copy-start.2 = (f32[6,128,1024]{1,2,0:T(8,128)}, f32[6,128,1024]{1,2,0:T(8,128)S(1)}, u32[]{:S(2)}) copy-start(f32[6,128,1024]{1,2,0:T(8,128)S(1)} %convolution_bitcast_fusion.12) | copy-start | bytes 9437188 | tf_op jit(solution)/shard_map/while
  76.0 1.9 %copy-start.6 = (bf16[2,128,512]{2,1,0:T(8,128)(2,1)S(1)}, bf16[2,128,512]{2,1,0:T(8,128)(2,1)}, u32[]{:S(2)}) copy-start(bf16[2,128,512]{2,1,0:T(8,128)(2,1)} %get-tuple-element.410) | copy-start | bytes 786436 | tf_op jit(solution)/shard_map/while
  77.9 3.6 %copy-start.7 = (bf16[2,128,512]{2,1,0:T(8,128)(2,1)}, bf16[2,128,512]{2,1,0:T(8,128)(2,1)S(1)}, u32[]{:S(2)}) copy-start(bf16[2,128,512]{2,1,0:T(8,128)(2,1)S(1)} %get-tuple-element.426) | copy-start | bytes 786436 | tf_op jit(solution)/shard_map/while
Sparse Core Ops, SparseCore 0:
  10.3 19.4 all-gather.2
  110.0 14.2 all-gather.4
where the time goes:
time: 134 us
  blocking collectives  30.8 us (23%)
  waiting for transfers between devices  27.6 us (21%)
  other arithmetic  22.2 us (17%)
  between operations  14.3 us (11%)
  matrix products  13.9 us (10%)
  starting transfers between devices  13.1 us (10%)
  local copies, waits for them, and re-layouts  11.7 us (9%)
    all_gather x1, waiting for transfers between devices, local(): lax.all_gather(settled, 'tile', axis=1, tiled=True)  14.5 us
    psum x1, blocking collectives, local(): lax.psum(grad_part.astype(jnp.bfloat16), 'tile').astype(jnp.float32)  10.4 us
    psum x1, blocking collectives, local(): spectra = lax.psum(partial_value.astype(jnp.bfloat16), 'tile')  10.4 us
    all_to_all x1, blocking collectives, local(): lax.all_to_all(returned.astype(jnp.bfloat16), 'ctx', split_axis=0, concat...  9.92 us
    sub x4, other arithmetic, complex_times(): factor_real * values_real - factor_imag * values_imag  8.65 us
    another operation x6, other arithmetic  7.55 us
    all_to_all x1, starting transfers between devices, local(): lax.all_to_all(wanted[:, None], 'ctx', split_axis=0, concat_axis=0, tiled...  7.31 us
    all_to_all x1, waiting for transfers between devices, local(): lax.all_to_all(outgoing, 'ctx', split_axis=0, concat_axis=0, tiled=True)  7.17 us
  transfers between devices with their start and end apart: 4, of which 4 were waited for; matrix products, arithmetic and copies ran while one was open for 5% of the time, Pallas kernels for 0%

commit v1 on v0

--- a/solution.py
+++ b/solution.py
@@ -203,12 +203,38 @@
         "mxy,yz->mxz", surface, blur_cols, preferred_element_type=jnp.float32
     ).astype(jnp.bfloat16)
     weights = own_blur_cols
-    mask_grad = jnp.einsum(
+    size, index, width_2 = (lax.axis_size("tile"), lax.axis_index("tile"), settled.shape[1])
+    upward = [(i, (i + 1) % size) for i in range(size)]
+    downward = [(i, (i - 1) % size) for i in range(size)]
+    halfway = size // 2
+    from_left = from_right = settled
+    running = jnp.einsum(
         "jx,mjz->mxz",
-        weights,
-        lax.all_gather(settled, "tile", axis=1, tiled=True),
+        lax.dynamic_slice_in_dim(weights, index * width_2, settled.shape[1], axis=0),
+        settled,
         preferred_element_type=jnp.float32,
     )
+    for turn in range(1, halfway + 1):
+        from_left = lax.ppermute(from_left, "tile", upward)
+        if turn < size - halfway:
+            from_right = lax.ppermute(from_right, "tile", downward)
+            running = running + jnp.einsum(
+                "jx,mjz->mxz",
+                lax.dynamic_slice_in_dim(
+                    weights, (index + turn) % size * width_2, from_right.shape[1], axis=0
+                ),
+                from_right,
+                preferred_element_type=jnp.float32,
+            )
+        running = running + jnp.einsum(
+            "jx,mjz->mxz",
+            lax.dynamic_slice_in_dim(
+                weights, (index - turn) % size * width_2, from_left.shape[1], axis=0
+            ),
+            from_left,
+            preferred_element_type=jnp.float32,
+        )
+    mask_grad = running
     return (resist, mask_grad)
 
 

time: 134 us -> 130 us (0.970)
  waiting for transfers between devices: 27.6 us -> 23.8 us
  starting transfers between devices: 13.1 us -> 14.8 us
    all_gather x1 -> x0, waiting for transfers between devices: 14.5 us -> none  [local(): lax.all_gather(settled, 'tile', axis=1, tiled=True)]
    ppermute x0 -> x3, waiting for transfers between devices: none -> 10.1 us  [the longest x2 9.72 us: local(): from_left = lax.ppermute(from_left, 'tile', upward)]
    ppermute x0 -> x3, starting transfers between devices: none -> 1.79 us  [the longest x1 1.73 us: local(): from_right = lax.ppermute(from_right, 'tile', downward)]
    unnamed x10 -> x12, local copies, waits for them, and re-layouts: 3.42 us -> 2.44 us
    while x16 -> x8, local copies, waits for them, and re-layouts: 4.44 us -> 4.43 us
  transfers between devices with their start and end apart: 4 -> 6, of which waited for: 4 -> 6; matrix products, arithmetic and copies ran while one was open for 5% -> 6% of each run, Pallas kernels for 0% -> 0%
where the time goes in v1:
time: 130 us
  blocking collectives  30.9 us (24%)
  waiting for transfers between devices  23.8 us (18%)
  other arithmetic  22.1 us (17%)
  starting transfers between devices  14.8 us (11%)
  between operations  14.4 us (11%)
  matrix products  12.9 us (10%)
  local copies, waits for them, and re-layouts  10.7 us (8%)
    psum x1, blocking collectives, local(): lax.psum(grad_part.astype(jnp.bfloat16), 'tile').astype(jnp.float32)  10.4 us
    psum x1, blocking collectives, local(): spectra = lax.psum(partial_value.astype(jnp.bfloat16), 'tile')  10.4 us
    all_to_all x1, blocking collectives, local(): lax.all_to_all(returned.astype(jnp.bfloat16), 'ctx', split_axis=0, concat...  10.1 us
    ppermute x2, waiting for transfers between devices, local(): from_left = lax.ppermute(from_left, 'tile', upward)  9.72 us
    sub x4, other arithmetic, complex_times(): factor_real * values_real - factor_imag * values_imag  8.64 us
    another operation x6, other arithmetic  7.55 us
    all_to_all x1, starting transfers between devices, local(): lax.all_to_all(wanted[:, None], 'ctx', split_axis=0, concat_axis=0, tiled...  7.31 us
    all_to_all x1, waiting for transfers between devices, local(): lax.all_to_all(outgoing, 'ctx', split_axis=0, concat_axis=0, tiled=True)  7.22 us
  transfers between devices with their start and end apart: 6, of which 6 were waited for; matrix products, arithmetic and copies ran while one was open for 6% of the time, Pallas kernels for 0%

profile of v1, /device:TPU:0, one launch (start us, length us, event | category | flops | bytes accessed | tf_op | source)
XLA Modules:
  0.0 129.9 jit_solution(5920911471340869207)
XLA Ops:
  7.2 2.2 %convolution_convert_fusion.4 = bf16[2,128,512]{2,1,0:T(8,128)(2,1)} fusion(bf16[2,128,512]{2,1,0:T(8,128)(2,1)} %param.9, bf16[512,512]{1,0:T(8,128)(2,1)} %param.11), kind=kOutput, calls=%fused_computation.60 | convolution fusion | flops 134348800 | bytes 1048576 | tf_op jit(solution)/shard_map/mxy,zy->mxz/dot_general | solution.py:133
  9.5 0.7 and_select_fusion.1
  10.4 0.7 copy.89
  11.1 7.3 %all-to-all-start = ((s32[8,1,1]{2,1,0:T(1,128)}), s32[8,1,1]{2,1,0:T(1,128)S(1)}, u32[]{:S(2)}, u32[]{:S(2)}) async-start(s32[8,1,1]{2,1,0:T(1,128)} %copy.89), calls=%async_computation | async-start | bytes 8192 | tf_op jit(solution)/shard_map/all_to_all | solution.py:129
  18.5 0.7 copy.87
  19.3 1.1 fusion.46
  20.7 0.6 fusion.64
  21.4 1.1 cosine_multiply_fusion
  22.9 2.0 %all-to-all-done = s32[8,1,1]{2,1,0:T(1,128)S(1)} async-done(((s32[8,1,1]{2,1,0:T(1,128)}), s32[8,1,1]{2,1,0:T(1,128)S(1)}, u32[]{:S(2)}, u32[]{:S(2)}) %all-to-all-start) | async-done | bytes 64 | tf_op jit(solution)/shard_map/all_to_all | solution.py:129
  24.8 0.2 reduce
  25.1 4.5 %all-gather.2.cloned.1.call-done = bf16[2,512,512]{2,1,0:T(8,128)(2,1)} async-done(((bf16[2,128,512]{2,1,0:T(8,128)(2,1)}), bf16[2,512,512]{2,1,0:T(8,128)(2,1)}) %all-gather.2.cloned.1.call-update) | async-done | bytes 1048592 | tf_op jit(solution)/shard_map/all_gather | solution.py:140
  29.6 1.9 %fusion.27 = bf16[2,128,128]{2,1,0:T(8,128)(2,1)S(1)} fusion(bf16[2,512,512]{2,1,0:T(8,128)(2,1)} %all-gather.2.cloned.1.call-done, bf16[512,128]{1,0:T(8,128)(2,1)S(1)} %maximum_convert_fusion, bf16[512,512]{1,0:T(8,128)(2,1)S(1)} %copy-done, s32[]{:T(128)S(6)} %select_n.172), kind=kOutput, calls=%fused_computation.68 | convolution fusion | flops 167936000 | bytes 1376260 | tf_op jit(solution)/shard_map/mxy,yv->mxv/dot_general | solution.py:143
  32.0 10.4 %psum.14 = bf16[2,64,128]{2,1,0:T(8,128)(2,1)S(1)} all-reduce(bf16[2,64,128]{2,1,0:T(8,128)(2,1)S(1)} %pad_maximum_fusion.1), channel_id=1, replica_groups=mesh['ctx'=8,'tile'=4] {'tile'}, use_global_device_ids=true, to_apply=%region_1.2 | all-reduce | flops 16384 | bytes 65536 | tf_op jit(solution)/shard_map/psum | solution.py:147
  42.4 0.3 convolution_convert_fusion.5
  42.7 0.7 copy.93
  43.4 5.7 %all-to-all-start.1 = ((bf16[8,64,128]{2,1,0:T(8,128)(2,1)}), bf16[8,64,128]{2,1,0:T(8,128)(2,1)S(1)}, u32[]{:S(2)}, u32[]{:S(2)}) async-start(bf16[8,64,128]{2,1,0:T(8,128)(2,1)} %copy.93), calls=%async_computation.1 | async-start | bytes 262144 | tf_op jit(solution)/shard_map/all_to_all | solution.py:151
  49.2 7.2 %all-to-all-done.1 = bf16[8,64,128]{2,1,0:T(8,128)(2,1)S(1)} async-done(((bf16[8,64,128]{2,1,0:T(8,128)(2,1)}), bf16[8,64,128]{2,1,0:T(8,128)(2,1)S(1)}, u32[]{:S(2)}, u32[]{:S(2)}) %all-to-all-start.1) | async-done | bytes 131104 | tf_op jit(solution)/shard_map/all_to_all | solution.py:151
  56.4 0.6 gather_fusion
  57.0 0.3 fusion.36
  57.3 4.6 %multiply_subtract_fusion.2 = (f32[24,64,64]{2,0,1:T(8,128)S(1)}, f32[24,64,64]{2,0,1:T(8,128)S(1)}) fusion(f32[24,64,128]{2,0,1:T(8,128)S(1)} %fusion.36, s32[24,64]{1,0:T(8,128)S(1)} %get-tuple-element.289, s32[24,64]{0,1:T(8,128)S(1)} %copy.88), kind=kLoop, calls=%fused_computation.82 | loop fusion | flops 2064384 | bytes 1585152 | tf_op jit(solution)/shard_map/sub | solution.py:64
  61.9 0.3 pad_maximum_fusion
  62.2 0.2 copy.95
  62.4 0.7 copy-done.5
  63.1 19.3 %while.14 = (s32[]{:T(128)}, bf16[2,128,512]{2,1,0:T(8,128)(2,1)S(1)}, bf16[2,64,128]{2,1,0:T(8,128)(2,1)S(1)}, f32[6,64,128]{2,1,0:T(8,128)S(1)}, f32[2,64,128]...) while((s32[]{:T(128)}, ...), condition=%wide.region_6.7_spmd, body=%wide.region_3.6_spmd.sunk | while | flops 538632192 | bytes 55263464 | solution.py:175
  63.3 0.4 convolution_convert_fusion.9
  63.8 0.6 convolution_bitcast_fusion.10
  64.4 0.6 convolution_bitcast_fusion.11
  65.0 1.0 copy-done.1
  66.0 0.4 add_reduce_fusion.2
  66.5 1.2 copy-done.2
  68.2 3.3 %multiply_convert_fusion.4 = (bf16[6,128,512]{1,2,0:T(8,128)(2,1)S(1)}, bf16[6,128,512]{1,2,0:T(8,128)(2,1)S(1)}) fusion(f32[128,512]{0,1:T(8,128)S(1)} %fusion.140, f32[6,128,1024]{1,2,0:T(8,128)} %copy-done.1, f32[6,128,1024]{1,2,0:T(8,128)} %copy-done.2), kind=kLoop, calls=%fused_computation.10.clone.1 | loop fusion | flops 2359296 | bytes 8126464 | tf_op jit(solution)/shard_map/convert
  71.5 0.6 fusion.141
  72.1 0.1 convolution_bitcast_fusion.12
  72.3 0.2 convolution_bitcast_fusion.13
  72.4 0.2 multiply_subtract_fusion.4
  73.0 0.4 convolution_convert_fusion.9
  73.4 0.6 convolution_bitcast_fusion.10
  74.1 0.6 convolution_bitcast_fusion.11
  74.7 1.0 copy-done.1
  75.7 0.4 add_reduce_fusion.2
  76.1 1.2 copy-done.2
  77.8 3.3 %multiply_convert_fusion.4 = (bf16[6,128,512]{1,2,0:T(8,128)(2,1)S(1)}, bf16[6,128,512]{1,2,0:T(8,128)(2,1)S(1)}) fusion(f32[128,512]{0,1:T(8,128)S(1)} %fusion.140, f32[6,128,1024]{1,2,0:T(8,128)} %copy-done.1, f32[6,128,1024]{1,2,0:T(8,128)} %copy-done.2), kind=kLoop, calls=%fused_computation.10.clone.1 | loop fusion | flops 2359296 | bytes 8126464 | tf_op jit(solution)/shard_map/convert
  81.1 0.6 fusion.141
  81.8 0.1 convolution_bitcast_fusion.12
  81.9 0.2 convolution_bitcast_fusion.13
  82.1 0.2 multiply_subtract_fusion.4
  82.4 10.4 %psum.15 = bf16[2,64,128]{2,1,0:T(8,128)(2,1)S(1)} all-reduce(bf16[2,64,128]{2,1,0:T(8,128)(2,1)S(1)} %get-tuple-element.159), channel_id=1, replica_groups=mesh['ctx'=8,'tile'=4] {'tile'}, use_global_device_ids=true, to_apply=%region_7.8 | all-reduce | flops 16384 | bytes 65536 | tf_op jit(solution)/shard_map/psum | solution.py:176
  93.0 0.3 fusion.101
  93.3 3.6 %multiply_subtract_fusion.1 = (f32[24,64,64]{2,0,1:T(8,128)S(1)}, f32[24,64,64]{2,0,1:T(8,128)S(1)}) fusion(f32[24,64,64]{2,1,0:T(8,128)S(1)} %get-tuple-element.276, f32[24,64,64]{2,1,0:T(8,128)S(1)} %get-tuple-element.275, s32[24,64]{1,0:T(8,128)S(1)} %get-tuple-element.289, s32[24,64]{0,1:T(8,128)S(1)} %copy.88), kind=kLoop, calls=%fused_computation.80 | loop fusion | flops 1966080 | bytes 1585152 | tf_op jit(solution)/shard_map/sub | solution.py:64
  96.9 0.5 convolution_convert_fusion.6
  97.5 10.1 %all_to_all.19 = bf16[8,64,128]{2,1,0:T(8,128)(2,1)S(1)} all-to-all(bf16[8,64,128]{2,1,0:T(8,128)(2,1)S(1)} %copy.101), channel_id=1, replica_groups=mesh['ctx'=8,'tile'=4] {'ctx'}, dimensions={0} | all-to-all | bytes 262144 | tf_op jit(solution)/shard_map/all_to_all | solution.py:185
  107.6 0.2 convolution_convert_fusion.7
  107.8 0.2 convolution_convert_fusion.2
  108.0 0.3 fusion.53
  108.3 0.6 convolution_convert_fusion.1
  109.0 1.7 %collective-permute-start = (bf16[2,128,512]{2,1,0:T(8,128)(2,1)S(1)}, bf16[2,128,512]{2,1,0:T(8,128)(2,1)S(1)}, u32[]{:S(2)}, u32[]{:S(2)}) collective-permute-start(bf16[2,128,512]{2,1,0:T(8,128)(2,1)S(1)} %convolution_convert_fusion.1), channel_id=1, source_target_pairs={{0,3},{1,0},{2,1},{3,2},{4,7},{5,4},{6,5},{7,6},{8,11},{9,8},{10,9... | collective-permute-start | bytes 786440 | tf_op jit(solution)/shard_map/ppermute | solution.py:220
  110.7 0.3 fusion.71
  111.0 5.0 %collective-permute-done.1 = bf16[2,128,512]{2,1,0:T(8,128)(2,1)S(1)} collective-permute-done((bf16[2,128,512]{2,1,0:T(8,128)(2,1)S(1)}, bf16[2,128,512]{2,1,0:T(8,128)(2,1)S(1)}, u32[]{:S(2)}, u32[]{:S(2)}) %collective-permute-start.1) | collective-permute-done | bytes 262176 | tf_op jit(solution)/shard_map/ppermute | solution.py:218
  116.0 0.4 collective-permute-done
  116.4 0.3 convolution_add_fusion.2
  116.7 0.3 convolution_add_fusion.1
  117.0 4.8 %collective-permute-done.2 = bf16[2,128,512]{2,1,0:T(8,128)(2,1)S(1)} collective-permute-done((bf16[2,128,512]{2,1,0:T(8,128)(2,1)S(1)}, bf16[2,128,512]{2,1,0:T(8,128)(2,1)S(1)}, u32[]{:S(2)}, u32[]{:S(2)}) %collective-permute-start.2) | collective-permute-done | bytes 262176 | tf_op jit(solution)/shard_map/ppermute | solution.py:218
  121.8 0.3 fusion.22
  122.1 1.0 copy.112
  (66 shorter events, 3.6 us)
Async XLA Ops:
  7.2 22.4 %copy-start = (bf16[512,512]{1,0:T(8,128)(2,1)S(1)}, bf16[512,512]{1,0:T(8,128)(2,1)}, u32[]{:S(2)}) copy-start(bf16[512,512]{1,0:T(8,128)(2,1)} %param.10) | copy-start | bytes 1572868
  7.2 22.4 %all-gather.2.cloned.1.call-start = ((), (), s32[]{:S(2)}) async-start(), calls=%async_computation.3 | async-start | bytes 1310720 | tf_op jit(solution)/shard_map/all_gather | solution.py:140
  11.1 13.7 %all-to-all-start = ((s32[8,1,1]{2,1,0:T(1,128)}), s32[8,1,1]{2,1,0:T(1,128)S(1)}, u32[]{:S(2)}, u32[]{:S(2)}) async-start(s32[8,1,1]{2,1,0:T(1,128)} %copy.89), calls=%async_computation | async-start | bytes 8192 | tf_op jit(solution)/shard_map/all_to_all | solution.py:129
  22.8 26.3 %copy-start.3 = (f32[6,64,128]{2,1,0:T(8,128)S(1)}, f32[6,64,128]{2,1,0:T(8,128)}, u32[]{:S(2)}) copy-start(f32[6,64,128]{2,1,0:T(8,128)} %param.12) | copy-start | bytes 589828
  43.4 13.0 %all-to-all-start.1 = ((bf16[8,64,128]{2,1,0:T(8,128)(2,1)}), bf16[8,64,128]{2,1,0:T(8,128)(2,1)S(1)}, u32[]{:S(2)}, u32[]{:S(2)}) async-start(bf16[8,64,128]{2,1,0:T(8,128)(2,1)} %copy.93), calls=%async_computation.1 | async-start | bytes 262144 | tf_op jit(solution)/shard_map/all_to_all | solution.py:151
  62.2 1.0 copy-start.5
  64.4 1.6 %copy-start.1 = (f32[6,128,1024]{1,2,0:T(8,128)}, f32[6,128,1024]{1,2,0:T(8,128)S(1)}, u32[]{:S(2)}) copy-start(f32[6,128,1024]{1,2,0:T(8,128)S(1)} %convolution_bitcast_fusion.10) | copy-start | bytes 9437188 | tf_op jit(solution)/shard_map/while
  66.0 1.7 %copy-start.2 = (f32[6,128,1024]{1,2,0:T(8,128)}, f32[6,128,1024]{1,2,0:T(8,128)S(1)}, u32[]{:S(2)}) copy-start(f32[6,128,1024]{1,2,0:T(8,128)S(1)} %convolution_bitcast_fusion.11) | copy-start | bytes 9437188 | tf_op jit(solution)/shard_map/while
  74.0 1.6 %copy-start.1 = (f32[6,128,1024]{1,2,0:T(8,128)}, f32[6,128,1024]{1,2,0:T(8,128)S(1)}, u32[]{:S(2)}) copy-start(f32[6,128,1024]{1,2,0:T(8,128)S(1)} %convolution_bitcast_fusion.10) | copy-start | bytes 9437188 | tf_op jit(solution)/shard_map/while
  75.7 1.7 %copy-start.2 = (f32[6,128,1024]{1,2,0:T(8,128)}, f32[6,128,1024]{1,2,0:T(8,128)S(1)}, u32[]{:S(2)}) copy-start(f32[6,128,1024]{1,2,0:T(8,128)S(1)} %convolution_bitcast_fusion.11) | copy-start | bytes 9437188 | tf_op jit(solution)/shard_map/while
  82.4 10.9 %copy-start.6 = (bf16[2,128,512]{2,1,0:T(8,128)(2,1)}, bf16[2,128,512]{2,1,0:T(8,128)(2,1)S(1)}, u32[]{:S(2)}) copy-start(bf16[2,128,512]{2,1,0:T(8,128)(2,1)S(1)} %get-tuple-element.233) | copy-start | bytes 786436
  97.5 10.8 %copy-start.4 = (bf16[512,512]{1,0:T(8,128)(2,1)S(1)}, bf16[512,512]{1,0:T(8,128)(2,1)}, u32[]{:S(2)}) copy-start(bf16[512,512]{1,0:T(8,128)(2,1)} %param.11) | copy-start | bytes 1572868
  108.9 7.1 %collective-permute-start.1 = (bf16[2,128,512]{2,1,0:T(8,128)(2,1)S(1)}, bf16[2,128,512]{2,1,0:T(8,128)(2,1)S(1)}, u32[]{:S(2)}, u32[]{:S(2)}) collective-permute-start(bf16[2,128,512]{2,1,0:T(8,128)(2,1)S(1)} %convolution_convert_fusion.1), channel_id=1, source_target_pairs={{0,1},{1,2},{2,3},{3,0},{4,5},{5,6},{6,7},{7,4},{8,9},{9,10},{10,1... | collective-permute-start | bytes 786440 | tf_op jit(solution)/shard_map/ppermute | solution.py:218
  109.0 7.4 %collective-permute-start = (bf16[2,128,512]{2,1,0:T(8,128)(2,1)S(1)}, bf16[2,128,512]{2,1,0:T(8,128)(2,1)S(1)}, u32[]{:S(2)}, u32[]{:S(2)}) collective-permute-start(bf16[2,128,512]{2,1,0:T(8,128)(2,1)S(1)} %convolution_convert_fusion.1), channel_id=1, source_target_pairs={{0,3},{1,0},{2,1},{3,2},{4,7},{5,4},{6,5},{7,6},{8,11},{9,8},{10,9... | collective-permute-start | bytes 786440 | tf_op jit(solution)/shard_map/ppermute | solution.py:220
  116.0 5.8 %collective-permute-start.2 = (bf16[2,128,512]{2,1,0:T(8,128)(2,1)S(1)}, bf16[2,128,512]{2,1,0:T(8,128)(2,1)S(1)}, u32[]{:S(2)}, u32[]{:S(2)}) collective-permute-start(bf16[2,128,512]{2,1,0:T(8,128)(2,1)S(1)} %collective-permute-done.1), channel_id=1, source_target_pairs={{0,1},{1,2},{2,3},{3,0},{4,5},{5,6},{6,7},{7,4},{8,9},{9,10},{10,1... | collective-permute-start | bytes 786440 | tf_op jit(solution)/shard_map/ppermute | solution.py:218
Sparse Core Ops, SparseCore 0:
  10.1 19.4 all-gather.1
